TPU v7x, 256 devices: a whole 4x4x8 slice. The times are simulated.
256 devices in a mesh: freq: 16 (over y, x), param: 4 (over z_hi, core), sens: 4 (over z_lo).
Axes of the slice: x: 4, y: 4, z: 8 (z_hi: 2, z_lo: 4; z = z_hi * 4 + z_lo), core: 2. Of those that a mesh axis runs over, the one named last changes fastest.
Arguments:
- series: bfloat16 [8, 600, 416], P(None, 'sens', 'freq'), may hold values from -6 to 6
- kernel: bfloat16 [2, 256, 600, 4096], P(None, 'freq', 'sens', 'param'), may hold values from -0.1875 to 0.1875
- prior_spectrum: float32 [256], P('freq'), may hold values from 0.3 to 1.5
- prior_scale: float32 [4096], P('param'), may hold values from 0.5 to 2
Outputs:
- adjoint_map: float32 [416, 8, 4096], P('freq', 'sens', 'param')
All inputs are finite; a program needn't handle non-finite values.
Results may differ from a plain program's by a relative error of at most 0.0047.
Values may be sent and summed in bfloat16 or wider, within the bound.
A program may use at most 64 MiB of HBM per device.

v0:
```python
import math
import jax
import jax.numpy as jnp
from jax import lax
from jax.sharding import PartitionSpec as P

LEN = 840
FB_DEV = 16


def joined_along(blocks, dim):
    blocks = jnp.moveaxis(blocks, 0, dim)
    lengths = blocks.shape
    return blocks.reshape(*lengths[:dim], lengths[dim] * lengths[dim + 1], *lengths[dim + 2 :])


def copy_for_each(x, axis):
    copies = jnp.broadcast_to(x, (lax.axis_size(axis), *x.shape))
    return lax.all_to_all(copies, axis, split_axis=0, concat_axis=0, tiled=True)


def gather_directly(x, axis, dim):
    return joined_along(copy_for_each(x, axis), dim)


def in_blocks(x, dim, count):
    before, after = (x.shape[:dim], x.shape[dim + 1 :])
    return jnp.moveaxis(x.reshape(*before, count, -1, *after), dim, 0)


def sent_and_summed(x, axis, dim):
    count = lax.axis_size(axis)
    blocks = lax.all_to_all(in_blocks(x, dim, count), axis, 0, 0, tiled=True)
    return jnp.sum(blocks.astype(jnp.float32), axis=0)


def extended(cells, sides, width):
    for axis, dim in sides:
        count = lax.axis_size(axis)
        ends = count - 1
        head = lax.slice_in_dim(cells, 0, width, axis=dim)
        tail = lax.slice_in_dim(cells, cells.shape[dim] - width, cells.shape[dim], axis=dim)
        cells = jnp.concatenate(
            [
                lax.ppermute(tail, axis, [(i, (i + 1) % count) for i in range(ends)]),
                cells,
                lax.ppermute(head, axis, [((i + 1) % count, i) for i in range(ends)]),
            ],
            axis=dim,
        )
    return cells


def phase_tables(bin_first, bin_count, time_count):
    bin_index = bin_first + jnp.arange(bin_count, dtype=jnp.int32)
    time_index = jnp.arange(time_count, dtype=jnp.int32)
    product = time_index[:, None] * bin_index[None, :] % LEN
    phase_angle = product.astype(jnp.float32) * (2.0 * math.pi / LEN)
    return (jnp.cos(phase_angle), jnp.sin(phase_angle))


def contract(spectrum, operator):
    return jnp.einsum("bsr,bsp->brp", spectrum, operator, preferred_element_type=jnp.float32)


def local(series, kernel, prior_spectrum, prior_scale):
    highest = lax.Precision.HIGHEST
    groups = lax.axis_size("freq")
    first_bin = lax.axis_index("freq") * FB_DEV
    probes, sens_dev, time_dev = series.shape
    total_times = time_dev * groups
    cosine, sine_part = phase_tables(first_bin, FB_DEV, total_times)
    phase_table = jnp.concatenate([cosine, -sine_part], axis=1)
    series_piece = gather_directly(series, "freq", 2)
    row_count = series_piece.shape[2]
    flat_rows = series_piece.astype(jnp.float32).reshape(-1, row_count)
    spectra = jnp.dot(flat_rows, phase_table, precision=highest)
    spectra = (spectra * (1.0 / math.sqrt(total_times))).astype(jnp.bfloat16)
    both_parts = (
        spectra.reshape(probes, sens_dev, 2, FB_DEV)
        .transpose(3, 1, 2, 0)
        .reshape(FB_DEV, sens_dev, 2 * probes)
    )
    with_real = contract(both_parts, kernel[0])
    with_imag = contract(both_parts, kernel[1])
    real_part = with_real[:, :probes] + with_imag[:, probes:]
    imag_part = with_real[:, probes:] - with_imag[:, :probes]
    partial_value = jnp.stack([real_part, imag_part])
    summed = sent_and_summed(partial_value.astype(jnp.bfloat16), "sens", 2)
    weights = prior_spectrum * (1.0 / math.sqrt(FB_DEV * groups))
    scaled_spec = summed * weights[None, :, None, None]
    arrived = lax.all_to_all(scaled_spec, "freq", split_axis=3, concat_axis=1, tiled=True)
    bin_total = arrived.shape[1]
    item_count = arrived.shape[2]
    col_count = arrived.shape[3]
    cos_all, sin_all = phase_tables(0, bin_total, total_times)
    full_table = jnp.concatenate([cos_all, -sin_all], axis=1)
    flat_rows = arrived.reshape(2 * bin_total, item_count * col_count)
    arranged = jnp.dot(full_table, flat_rows, precision=highest).reshape(
        total_times, item_count, col_count
    )
    image_field = lax.all_to_all(arranged, "freq", split_axis=0, concat_axis=2, tiled=True)
    weighted = image_field * prior_scale
    padded = extended(weighted.astype(jnp.bfloat16), (("param", 2),), 1).astype(weighted.dtype)
    smooth = 0.5 * weighted + 0.25 * (padded[:, :, :-2] + padded[:, :, 2:])
    return smooth * prior_scale


def solution(mesh):
    placed = (P(None, "sens", "freq"), P(None, "freq", "sens", "param"), P("freq"), P("param"))
    return jax.shard_map(
        local, mesh=mesh, in_specs=placed, out_specs=P("freq", "sens", "param"), check_vma=False
    )
```

profile of v0, /device:TPU:1, one launch (start us, length us, event | category | flops | bytes accessed | tf_op | source)
XLA Modules:
  0.0 131.3 jit_solution(14938299021006991970)
XLA Ops:
  0.0 2.2 %broadcast_in_dim.2 = bf16[16,8,150,26]{2,1,3,0:T(8,128)(2,1)} broadcast(bf16[8,150,26]{1,0,2:T(8,128)(2,1)} %param.4), dimensions={1,2,3} | broadcast | bytes 1060800 | tf_op jit(solution)/shard_map/broadcast_in_dim | solution.py:18
  2.2 7.6 %all-to-all-start = ((bf16[16,8,150,26]{2,1,3,0:T(8,128)(2,1)}), bf16[16,8,150,26]{2,1,3,0:T(8,128)(2,1)S(1)}, u32[]{:S(2)}, u32[]{:S(2)}) async-start(bf16[16,8,150,26]{2,1,3,0:T(8,128)(2,1)} %broadcast_in_dim.2), calls=%async_computation | async-start | bytes 3407872 | tf_op jit(solution)/shard_map/all_to_all | solution.py:19
  10.0 9.9 %fusion.33 = (bf16[1,16,150,1024]{3,1,2,0:T(8,128)(2,1)}, bf16[1,16,150,1024]{3,1,2,0:T(8,128)(2,1)}) fusion(bf16[2,16,150,1024]{3,1,2,0:T(8,128)(2,1)} %param.5), kind=kLoop, calls=%fused_computation.53 | loop fusion | bytes 19660800 | tf_op jit(solution)/shard_map/slice | solution.py:84
  20.0 14.8 %all-to-all-done = bf16[16,8,150,26]{2,1,3,0:T(8,128)(2,1)S(1)} async-done(((bf16[16,8,150,26]{2,1,3,0:T(8,128)(2,1)}), bf16[16,8,150,26]{2,1,3,0:T(8,128)(2,1)S(1)}, u32[]{:S(2)}, u32[]{:S(2)}) %all-to-all-start) | async-done | bytes 998432 | tf_op jit(solution)/shard_map/all_to_all | solution.py:19
  34.8 1.9 %reshape.30 = bf16[1200,416]{0,1:T(8,128)(2,1)S(1)} reshape(bf16[8,150,16,26]{1,0,3,2:T(8,128)(2,1)S(1)} %bitcast.47) | data formatting | bytes 1996800 | tf_op jit(solution)/shard_map/reshape | solution.py:76
  36.8 0.5 fusion.3
  37.5 8.0 %fusion.1 = f32[16,16,1024]{2,1,0:T(8,128)S(1)} fusion(bf16[1,16,150,1024]{3,1,2,0:T(8,128)(2,1)} %get-tuple-element.5, bf16[8,150,2,16]{1,0,3,2:T(8,128)(2,1)S(1)} %reshape.31), kind=kOutput, calls=%fused_computation.3 | convolution fusion | flops 78643200 | bytes 6040576 | tf_op jit(solution)/shard_map/bsr,bsp->brp/dot_general | solution.py:63
  45.5 5.4 %fusion = f32[16,16,1024]{2,1,0:T(8,128)S(1)} fusion(bf16[1,16,150,1024]{3,1,2,0:T(8,128)(2,1)S(1)} %copy-done, bf16[8,150,2,16]{1,0,3,2:T(8,128)(2,1)S(1)} %reshape.31), kind=kOutput, calls=%fused_computation.1 | convolution fusion | flops 78643200 | bytes 6040576 | tf_op jit(solution)/shard_map/bsr,bsp->brp/dot_general | solution.py:63
  51.2 0.3 stack.9
  51.6 1.3 %copy_bitcast_fusion.4 = bf16[4,2,16,2,1024]{4,3,2,1,0:T(2,128)(2,1)} fusion(bf16[1,16,4,2,1024]{4,3,2,1,0:T(2,128)(2,1)S(1)} %stack.10, bf16[1,16,4,2,1024]{4,3,2,1,0:T(2,128)(2,1)S(1)} %stack.9), kind=kLoop, calls=%fused_computation.18 | loop fusion | flops 262144 | bytes 1048576 | tf_op jit(solution)/shard_map/transpose | solution.py:28
  52.9 5.6 %all-to-all-start.1 = ((bf16[4,2,16,2,1024]{4,3,2,1,0:T(2,128)(2,1)}), bf16[4,2,16,2,1024]{4,3,2,1,0:T(2,128)(2,1)S(1)}, u32[]{:S(2)}, u32[]{:S(2)}) async-start(bf16[4,2,16,2,1024]{4,3,2,1,0:T(2,128)(2,1)} %copy_bitcast_fusion.4), calls=%async_computation.1 | async-start | bytes 1048576 | tf_op jit(solution)/shard_map/all_to_all | solution.py:33
  58.5 13.3 %all-to-all-done.1 = bf16[4,2,16,2,1024]{4,3,2,1,0:T(2,128)(2,1)S(1)} async-done(((bf16[4,2,16,2,1024]{4,3,2,1,0:T(2,128)(2,1)}), bf16[4,2,16,2,1024]{4,3,2,1,0:T(2,128)(2,1)S(1)}, u32[]{:S(2)}, u32[]{:S(2)}) %all-to-all-start.1) | async-done | bytes 524320 | tf_op jit(solution)/shard_map/all_to_all | solution.py:33
  72.0 1.3 %copy.43 = f32[2,16,2,1024]{1,2,0,3:T(2,128)S(1)} copy(f32[2,16,2,1024]{3,1,2,0:T(8,128)S(1)} %broadcast_multiply_fusion) | data formatting | bytes 524288 | tf_op jit(solution)/shard_map/mul | solution.py:91
  73.3 3.6 %reshape.35 = f32[16,1,4096]{2,1,0:T(1,128)} reshape(f32[1024,2,2,16]{3,2,1,0:T(2,128)S(1)} %bitcast.46) | data formatting | bytes 524288
  76.9 5.1 %all-to-all-start.2 = ((f32[16,1,4096]{2,1,0:T(1,128)}), f32[16,1,4096]{2,1,0:T(1,128)S(1)}, u32[]{:S(2)}, u32[]{:S(2)}) async-start(f32[16,1,4096]{2,1,0:T(1,128)} %reshape.35), calls=%async_computation.2 | async-start | bytes 524288 | tf_op jit(solution)/shard_map/all_to_all | solution.py:92
  82.1 1.8 %sine_negate_fusion = (f32[416,256]{1,0:T(8,128)S(1)}, f32[416,256]{1,0:T(8,128)S(1)}) fusion(), kind=kLoop, calls=%fused_computation.21 | loop fusion | flops 1064960 | bytes 851968 | tf_op jit(solution)/shard_map/neg | solution.py:97
  83.9 5.9 %all-to-all-done.2 = f32[16,1,4096]{2,1,0:T(1,128)S(1)} async-done(((f32[16,1,4096]{2,1,0:T(1,128)}), f32[16,1,4096]{2,1,0:T(1,128)S(1)}, u32[]{:S(2)}, u32[]{:S(2)}) %all-to-all-start.2) | async-done | bytes 262176 | tf_op jit(solution)/shard_map/all_to_all | solution.py:92
  89.7 0.5 broadcast.17
  90.2 1.3 reduce
  91.5 2.8 %reshape.36 = f32[1024,2,2,16]{3,2,1,0:T(2,128)S(1)} reshape(f32[16,4096]{1,0:T(8,128)S(1)} %reduce) | data formatting | bytes 524288
  94.3 1.5 %copy.50 = f32[2,16,2,16,64]{4,3,1,2,0:T(8,128)S(1)} copy(f32[2,16,2,16,64]{1,2,0,4,3:T(2,128)S(1)} %bitcast.45) | data formatting | bytes 524288 | tf_op jit(solution)/shard_map/all_to_all | solution.py:92
  95.9 0.4 copy.45
  96.3 0.3 reshape.33
  96.7 0.9 fusion.4
  97.9 0.4 reshape.37
  98.3 10.1 %all_to_all.43 = f32[16,1,3328]{2,1,0:T(1,128)S(1)} all-to-all(f32[16,1,3328]{2,1,0:T(1,128)S(1)} %reshape.37), channel_id=1, replica_groups=mesh['freq'=16,'param'=4,'sens'=4] {'freq'}, dimensions={0} | all-to-all | bytes 425984 | tf_op jit(solution)/shard_map/all_to_all | solution.py:102
  108.4 1.1 reduce.1
  110.3 10.5 %collective-permute-start = (bf16[26,2,1]{2,1,0:T(2,128)(2,1)S(1)}, bf16[26,2,1]{2,1,0:T(2,128)(2,1)S(1)}, u32[]{:S(2)}, u32[]{:S(2)}) collective-permute-start(bf16[26,2,1]{2,1,0:T(2,128)(2,1)S(1)} %get-tuple-element.10), channel_id=1, source_target_pairs={{0,4},{4,8},{8,12},{1,5},{5,9},{9,13},{2,6},{6,10},{10,14},{3,7},{... | collective-permute-start | bytes 320 | tf_op jit(solution)/shard_map/ppermute | solution.py:45
  120.8 1.9 %collective-permute-start.1 = (bf16[26,2,1]{2,1,0:T(2,128)(2,1)S(1)}, bf16[26,2,1]{2,1,0:T(2,128)(2,1)S(1)}, u32[]{:S(2)}, u32[]{:S(2)}) collective-permute-start(bf16[26,2,1]{2,1,0:T(2,128)(2,1)S(1)} %get-tuple-element.9), channel_id=1, source_target_pairs={{4,0},{8,4},{12,8},{5,1},{9,5},{13,9},{6,2},{10,6},{14,10},{7,3},{... | collective-permute-start | bytes 320 | tf_op jit(solution)/shard_map/ppermute | solution.py:47
  122.8 7.0 %collective-permute-done.1 = bf16[26,2,1]{2,1,0:T(2,128)(2,1)S(1)} collective-permute-done((bf16[26,2,1]{2,1,0:T(2,128)(2,1)S(1)}, bf16[26,2,1]{2,1,0:T(2,128)(2,1)S(1)}, u32[]{:S(2)}, u32[]{:S(2)}) %collective-permute-start.1) | collective-permute-done | bytes 136 | tf_op jit(solution)/shard_map/ppermute | solution.py:47
  129.8 0.5 concatenate.13
  130.3 1.0 fusion.17
  (23 shorter events, 2.1 us)
Async XLA Ops:
  2.2 32.6 %all-to-all-start = ((bf16[16,8,150,26]{2,1,3,0:T(8,128)(2,1)}), bf16[16,8,150,26]{2,1,3,0:T(8,128)(2,1)S(1)}, u32[]{:S(2)}, u32[]{:S(2)}) async-start(bf16[16,8,150,26]{2,1,3,0:T(8,128)(2,1)} %broadcast_in_dim.2), calls=%async_computation | async-start | bytes 3407872 | tf_op jit(solution)/shard_map/all_to_all | solution.py:19
  37.5 8.0 %copy-start = (bf16[1,16,150,1024]{3,1,2,0:T(8,128)(2,1)S(1)}, bf16[1,16,150,1024]{3,1,2,0:T(8,128)(2,1)}, u32[]{:S(2)}) copy-start(bf16[1,16,150,1024]{3,1,2,0:T(8,128)(2,1)} %get-tuple-element.6) | copy-start | bytes 14745604
  45.5 13.0 %copy-start.2 = (f32[16]{0:T(128)S(1)}, f32[16]{0:T(128)}, u32[]{:S(2)}) copy-start(f32[16]{0:T(128)} %param.6) | copy-start | bytes 196
  52.9 18.9 %all-to-all-start.1 = ((bf16[4,2,16,2,1024]{4,3,2,1,0:T(2,128)(2,1)}), bf16[4,2,16,2,1024]{4,3,2,1,0:T(2,128)(2,1)S(1)}, u32[]{:S(2)}, u32[]{:S(2)}) async-start(bf16[4,2,16,2,1024]{4,3,2,1,0:T(2,128)(2,1)} %copy_bitcast_fusion.4), calls=%async_computation.1 | async-start | bytes 1048576 | tf_op jit(solution)/shard_map/all_to_all | solution.py:33
  76.9 12.8 %all-to-all-start.2 = ((f32[16,1,4096]{2,1,0:T(1,128)}), f32[16,1,4096]{2,1,0:T(1,128)S(1)}, u32[]{:S(2)}, u32[]{:S(2)}) async-start(f32[16,1,4096]{2,1,0:T(1,128)} %reshape.35), calls=%async_computation.2 | async-start | bytes 524288 | tf_op jit(solution)/shard_map/all_to_all | solution.py:92
  94.3 15.8 %copy-start.1 = (f32[1024]{0:T(1024)S(1)}, f32[1024]{0:T(1024)}, u32[]{:S(2)}) copy-start(f32[1024]{0:T(1024)} %param.7) | copy-start | bytes 12292
  110.3 12.4 %collective-permute-start = (bf16[26,2,1]{2,1,0:T(2,128)(2,1)S(1)}, bf16[26,2,1]{2,1,0:T(2,128)(2,1)S(1)}, u32[]{:S(2)}, u32[]{:S(2)}) collective-permute-start(bf16[26,2,1]{2,1,0:T(2,128)(2,1)S(1)} %get-tuple-element.10), channel_id=1, source_target_pairs={{0,4},{4,8},{8,12},{1,5},{5,9},{9,13},{2,6},{6,10},{10,14},{3,7},{... | collective-permute-start | bytes 320 | tf_op jit(solution)/shard_map/ppermute | solution.py:45
  120.8 8.9 %collective-permute-start.1 = (bf16[26,2,1]{2,1,0:T(2,128)(2,1)S(1)}, bf16[26,2,1]{2,1,0:T(2,128)(2,1)S(1)}, u32[]{:S(2)}, u32[]{:S(2)}) collective-permute-start(bf16[26,2,1]{2,1,0:T(2,128)(2,1)S(1)} %get-tuple-element.9), channel_id=1, source_target_pairs={{4,0},{8,4},{12,8},{5,1},{9,5},{13,9},{6,2},{10,6},{14,10},{7,3},{... | collective-permute-start | bytes 320 | tf_op jit(solution)/shard_map/ppermute | solution.py:47
where the time goes:
time: 132 us; the launch traced here: 131 us
  waiting for transfers between devices  41 us (31%)
  starting transfers between devices  30.7 us (23%)
  local copies, waits for them, and re-layouts  27.1 us (21%)
  matrix products  14.8 us (11%)
  blocking collectives  10.1 us (8%)
  other arithmetic  7.26 us (6%)
    all_to_all x1, waiting for transfers between devices, copy_for_each(): return lax.all_to_all(copies, axis, split_axis=0, concat_axis=0, tiled=True)  14.8 us
    dot_general x2, matrix products, contract(): jnp.einsum('bsr,bsp->brp', spectrum, operator, preferred_element_type=jnp...  13.4 us
    all_to_all x1, waiting for transfers between devices, sent_and_summed(): blocks = lax.all_to_all(in_blocks(x, dim, count), axis, 0, 0, tiled=True)  13.3 us
    ppermute x1, starting transfers between devices, extended(): lax.ppermute(tail, axis, [(i, (i + 1) % count) for i in range(ends)])  10.5 us
    all_to_all x1, blocking collectives, local(): lax.all_to_all(arranged, 'freq', split_axis=0, concat_axis=2, tiled=True)  10.1 us
    slice x1, local copies, waits for them, and re-layouts, local(): with_real = contract(both_parts, kernel[0])  9.95 us
    all_to_all x1, starting transfers between devices, copy_for_each(): return lax.all_to_all(copies, axis, split_axis=0, concat_axis=0, tiled=True)  7.57 us
    unnamed x10, local copies, waits for them, and re-layouts  7.13 us
  transfers between devices with their start and end apart: 5, of which 4 were waited for; matrix products, arithmetic and copies ran while one was open for 9% of the time, Pallas kernels for 0%

commit v1 on v0

--- a/solution.py
+++ b/solution.py
@@ -89,7 +89,9 @@
     summed = sent_and_summed(partial_value.astype(jnp.bfloat16), "sens", 2)
     weights = prior_spectrum * (1.0 / math.sqrt(FB_DEV * groups))
     scaled_spec = summed * weights[None, :, None, None]
-    arrived = lax.all_to_all(scaled_spec, "freq", split_axis=3, concat_axis=1, tiled=True)
+    parts = jnp.split(scaled_spec, lax.axis_size("freq"), axis=3)
+    incoming = lax.all_to_all(jnp.stack(parts), "freq", 0, 0)
+    arrived = jnp.concatenate(incoming, axis=1)
     bin_total = arrived.shape[1]
     item_count = arrived.shape[2]
     col_count = arrived.shape[3]

time: 132 us -> 125 us (0.947)
  local copies, waits for them, and re-layouts: 27.1 us -> 20.2 us
    unnamed x10 -> x25, local copies, waits for them, and re-layouts: 7.13 us -> 3.34 us
    all_to_all x3 -> x1, local copies, waits for them, and re-layouts: 2.46 us -> 0.51 us  [local(): incoming = lax.all_to_all(jnp.stack(parts), 'freq', 0, 0)]
    mul x1 -> x0, local copies, waits for them, and re-layouts: 1.35 us -> none  [local(): scaled_spec = summed * weights[None, :, None, None]]
  transfers between devices with their start and end apart: 5 -> 5, of which waited for: 4 -> 4; matrix products, arithmetic and copies ran while one was open for 9% -> 10% of each run, Pallas kernels for 0% -> 0%
where the time goes in v1:
time: 125 us
  waiting for transfers between devices  41 us (33%)
  starting transfers between devices  30.7 us (25%)
  local copies, waits for them, and re-layouts  20.2 us (16%)
  matrix products  14.8 us (12%)
  blocking collectives  10.1 us (8%)
  other arithmetic  7.74 us (6%)
    all_to_all x1, waiting for transfers between devices, copy_for_each(): return lax.all_to_all(copies, axis, split_axis=0, concat_axis=0, tiled=True)  14.8 us
    dot_general x2, matrix products, contract(): jnp.einsum('bsr,bsp->brp', spectrum, operator, preferred_element_type=jnp...  13.4 us
    all_to_all x1, waiting for transfers between devices, sent_and_summed(): blocks = lax.all_to_all(in_blocks(x, dim, count), axis, 0, 0, tiled=True)  13.3 us
    ppermute x1, starting transfers between devices, extended(): lax.ppermute(tail, axis, [(i, (i + 1) % count) for i in range(ends)])  10.5 us
    all_to_all x1, blocking collectives, local(): lax.all_to_all(arranged, 'freq', split_axis=0, concat_axis=2, tiled=True)  10.1 us
    slice x1, local copies, waits for them, and re-layouts, local(): with_real = contract(both_parts, kernel[0])  9.95 us
    all_to_all x1, starting transfers between devices, copy_for_each(): return lax.all_to_all(copies, axis, split_axis=0, concat_axis=0, tiled=True)  7.57 us
    ppermute x1, waiting for transfers between devices, extended(): lax.ppermute(head, axis, [((i + 1) % count, i) for i in range(ends)])  6.99 us
  transfers between devices with their start and end apart: 5, of which 4 were waited for; matrix products, arithmetic and copies ran while one was open for 10% of the time, Pallas kernels for 0%

profile of v1, /device:TPU:1, one launch (start us, length us, event | category | flops | bytes accessed | tf_op | source)
XLA Modules:
  0.0 124.9 jit_solution(4804011337673413131)
XLA Ops:
  0.0 2.2 %broadcast_in_dim.2 = bf16[16,8,150,26]{2,1,3,0:T(8,128)(2,1)} broadcast(bf16[8,150,26]{1,0,2:T(8,128)(2,1)} %param.4), dimensions={1,2,3} | broadcast | bytes 1060800 | tf_op jit(solution)/shard_map/broadcast_in_dim | solution.py:18
  2.2 7.6 %all-to-all-start = ((bf16[16,8,150,26]{2,1,3,0:T(8,128)(2,1)}), bf16[16,8,150,26]{2,1,3,0:T(8,128)(2,1)S(1)}, u32[]{:S(2)}, u32[]{:S(2)}) async-start(bf16[16,8,150,26]{2,1,3,0:T(8,128)(2,1)} %broadcast_in_dim.2), calls=%async_computation | async-start | bytes 3407872 | tf_op jit(solution)/shard_map/all_to_all | solution.py:19
  10.0 9.9 %fusion.33 = (bf16[1,16,150,1024]{3,1,2,0:T(8,128)(2,1)}, bf16[1,16,150,1024]{3,1,2,0:T(8,128)(2,1)}) fusion(bf16[2,16,150,1024]{3,1,2,0:T(8,128)(2,1)} %param.5), kind=kLoop, calls=%fused_computation.85 | loop fusion | bytes 19660800 | tf_op jit(solution)/shard_map/slice | solution.py:84
  20.0 14.8 %all-to-all-done = bf16[16,8,150,26]{2,1,3,0:T(8,128)(2,1)S(1)} async-done(((bf16[16,8,150,26]{2,1,3,0:T(8,128)(2,1)}), bf16[16,8,150,26]{2,1,3,0:T(8,128)(2,1)S(1)}, u32[]{:S(2)}, u32[]{:S(2)}) %all-to-all-start) | async-done | bytes 998432 | tf_op jit(solution)/shard_map/all_to_all | solution.py:19
  34.8 1.9 %reshape.29 = bf16[1200,416]{0,1:T(8,128)(2,1)S(1)} reshape(bf16[8,150,16,26]{1,0,3,2:T(8,128)(2,1)S(1)} %bitcast.106) | data formatting | bytes 1996800 | tf_op jit(solution)/shard_map/reshape | solution.py:76
  36.8 0.5 fusion.3
  37.5 8.0 %fusion.1 = f32[16,16,1024]{2,1,0:T(8,128)S(1)} fusion(bf16[1,16,150,1024]{3,1,2,0:T(8,128)(2,1)} %get-tuple-element.5, bf16[8,150,2,16]{1,0,3,2:T(8,128)(2,1)S(1)} %reshape.30), kind=kOutput, calls=%fused_computation.3 | convolution fusion | flops 78643200 | bytes 6040576 | tf_op jit(solution)/shard_map/bsr,bsp->brp/dot_general | solution.py:63
  45.5 5.4 %fusion = f32[16,16,1024]{2,1,0:T(8,128)S(1)} fusion(bf16[1,16,150,1024]{3,1,2,0:T(8,128)(2,1)S(1)} %copy-done, bf16[8,150,2,16]{1,0,3,2:T(8,128)(2,1)S(1)} %reshape.30), kind=kOutput, calls=%fused_computation.1 | convolution fusion | flops 78643200 | bytes 6040576 | tf_op jit(solution)/shard_map/bsr,bsp->brp/dot_general | solution.py:63
  51.2 0.3 stack.61
  51.6 1.3 %copy_bitcast_fusion.4 = bf16[4,2,16,2,1024]{4,3,2,1,0:T(2,128)(2,1)} fusion(bf16[1,16,4,2,1024]{4,3,2,1,0:T(2,128)(2,1)S(1)} %stack.61, bf16[1,16,4,2,1024]{4,3,2,1,0:T(2,128)(2,1)S(1)} %stack.60), kind=kLoop, calls=%fused_computation.18 | loop fusion | flops 262144 | bytes 1048576 | tf_op jit(solution)/shard_map/transpose | solution.py:28
  52.9 5.6 %all-to-all-start.1 = ((bf16[4,2,16,2,1024]{4,3,2,1,0:T(2,128)(2,1)}), bf16[4,2,16,2,1024]{4,3,2,1,0:T(2,128)(2,1)S(1)}, u32[]{:S(2)}, u32[]{:S(2)}) async-start(bf16[4,2,16,2,1024]{4,3,2,1,0:T(2,128)(2,1)} %copy_bitcast_fusion.4), calls=%async_computation.1 | async-start | bytes 1048576 | tf_op jit(solution)/shard_map/all_to_all | solution.py:33
  58.5 13.3 %all-to-all-done.1 = bf16[4,2,16,2,1024]{4,3,2,1,0:T(2,128)(2,1)S(1)} async-done(((bf16[4,2,16,2,1024]{4,3,2,1,0:T(2,128)(2,1)}), bf16[4,2,16,2,1024]{4,3,2,1,0:T(2,128)(2,1)S(1)}, u32[]{:S(2)}, u32[]{:S(2)}) %all-to-all-start.1) | async-done | bytes 524320 | tf_op jit(solution)/shard_map/all_to_all | solution.py:33
  71.8 0.5 convert_reduce_fusion
  73.6 1.3 %reshape.34 = f32[16,1,4096]{2,1,0:T(1,128)} reshape(f32[16,2,16,2,64]{4,3,2,1,0:T(2,128)S(1)} %constant_dynamic-update-slice_fusion) | data formatting | bytes 524288
  74.9 5.1 %all-to-all-start.2 = ((f32[16,1,4096]{2,1,0:T(1,128)}), f32[16,1,4096]{2,1,0:T(1,128)S(1)}, u32[]{:S(2)}, u32[]{:S(2)}) async-start(f32[16,1,4096]{2,1,0:T(1,128)} %reshape.34), calls=%async_computation.2 | async-start | bytes 524288 | tf_op jit(solution)/shard_map/all_to_all | solution.py:93
  80.0 1.8 %sine_negate_fusion = (f32[416,256]{1,0:T(8,128)S(1)}, f32[416,256]{1,0:T(8,128)S(1)}) fusion(), kind=kLoop, calls=%fused_computation.21 | loop fusion | flops 1064960 | bytes 851968 | tf_op jit(solution)/shard_map/neg | solution.py:99
  81.8 5.8 %all-to-all-done.2 = f32[16,1,4096]{2,1,0:T(1,128)S(1)} async-done(((f32[16,1,4096]{2,1,0:T(1,128)}), f32[16,1,4096]{2,1,0:T(1,128)S(1)}, u32[]{:S(2)}, u32[]{:S(2)}) %all-to-all-start.2) | async-done | bytes 262176 | tf_op jit(solution)/shard_map/all_to_all | solution.py:93
  87.7 0.5 broadcast.17
  88.2 1.3 %reduce = f32[16,4096]{1,0:T(8,128)S(1)} reduce(f32[16,1,4096]{2,1,0:T(1,128)S(1)} %all-to-all-done.2, f32[]{:T(128)} %broadcast.17), dimensions={1}, to_apply=%all_to_all.24.reduce_sub_computation | reduce | bytes 524292 | tf_op jit(solution)/shard_map/all_to_all | solution.py:93
  89.4 0.4 reshape.35
  89.9 0.3 reshape_reshape.3
  90.3 0.9 fusion.4
  91.5 0.4 reshape.36
  91.9 10.1 %all_to_all.33 = f32[16,1,3328]{2,1,0:T(1,128)S(1)} all-to-all(f32[16,1,3328]{2,1,0:T(1,128)S(1)} %reshape.36), channel_id=1, replica_groups=mesh['freq'=16,'param'=4,'sens'=4] {'freq'}, dimensions={0} | all-to-all | bytes 425984 | tf_op jit(solution)/shard_map/all_to_all | solution.py:104
  102.0 1.1 reduce.1
  103.2 0.3 reshape.37
  103.5 0.2 all_to_all.28
  103.9 10.5 %collective-permute-start = (bf16[26,2,1]{2,1,0:T(2,128)(2,1)S(1)}, bf16[26,2,1]{2,1,0:T(2,128)(2,1)S(1)}, u32[]{:S(2)}, u32[]{:S(2)}) collective-permute-start(bf16[26,2,1]{2,1,0:T(2,128)(2,1)S(1)} %get-tuple-element.10), channel_id=1, source_target_pairs={{0,4},{4,8},{8,12},{1,5},{5,9},{9,13},{2,6},{6,10},{10,14},{3,7},{... | collective-permute-start | bytes 320 | tf_op jit(solution)/shard_map/ppermute | solution.py:45
  114.4 1.9 %collective-permute-start.1 = (bf16[26,2,1]{2,1,0:T(2,128)(2,1)S(1)}, bf16[26,2,1]{2,1,0:T(2,128)(2,1)S(1)}, u32[]{:S(2)}, u32[]{:S(2)}) collective-permute-start(bf16[26,2,1]{2,1,0:T(2,128)(2,1)S(1)} %get-tuple-element.9), channel_id=1, source_target_pairs={{4,0},{8,4},{12,8},{5,1},{9,5},{13,9},{6,2},{10,6},{14,10},{7,3},{... | collective-permute-start | bytes 320 | tf_op jit(solution)/shard_map/ppermute | solution.py:47
  116.4 7.0 %collective-permute-done.1 = bf16[26,2,1]{2,1,0:T(2,128)(2,1)S(1)} collective-permute-done((bf16[26,2,1]{2,1,0:T(2,128)(2,1)S(1)}, bf16[26,2,1]{2,1,0:T(2,128)(2,1)S(1)}, u32[]{:S(2)}, u32[]{:S(2)}) %collective-permute-start.1) | collective-permute-done | bytes 136 | tf_op jit(solution)/shard_map/ppermute | solution.py:47
  123.4 0.5 concatenate.13
  123.9 1.0 fusion.17
  (37 shorter events, 2.7 us)
Async XLA Ops:
  2.2 32.6 %all-to-all-start = ((bf16[16,8,150,26]{2,1,3,0:T(8,128)(2,1)}), bf16[16,8,150,26]{2,1,3,0:T(8,128)(2,1)S(1)}, u32[]{:S(2)}, u32[]{:S(2)}) async-start(bf16[16,8,150,26]{2,1,3,0:T(8,128)(2,1)} %broadcast_in_dim.2), calls=%async_computation | async-start | bytes 3407872 | tf_op jit(solution)/shard_map/all_to_all | solution.py:19
  37.5 8.0 %copy-start = (bf16[1,16,150,1024]{3,1,2,0:T(8,128)(2,1)S(1)}, bf16[1,16,150,1024]{3,1,2,0:T(8,128)(2,1)}, u32[]{:S(2)}) copy-start(bf16[1,16,150,1024]{3,1,2,0:T(8,128)(2,1)} %get-tuple-element.6) | copy-start | bytes 14745604
  45.5 13.0 %copy-start.2 = (f32[16]{0:T(128)S(1)}, f32[16]{0:T(128)}, u32[]{:S(2)}) copy-start(f32[16]{0:T(128)} %param.6) | copy-start | bytes 196
  52.9 18.9 %all-to-all-start.1 = ((bf16[4,2,16,2,1024]{4,3,2,1,0:T(2,128)(2,1)}), bf16[4,2,16,2,1024]{4,3,2,1,0:T(2,128)(2,1)S(1)}, u32[]{:S(2)}, u32[]{:S(2)}) async-start(bf16[4,2,16,2,1024]{4,3,2,1,0:T(2,128)(2,1)} %copy_bitcast_fusion.4), calls=%async_computation.1 | async-start | bytes 1048576 | tf_op jit(solution)/shard_map/all_to_all | solution.py:33
  74.9 12.8 %all-to-all-start.2 = ((f32[16,1,4096]{2,1,0:T(1,128)}), f32[16,1,4096]{2,1,0:T(1,128)S(1)}, u32[]{:S(2)}, u32[]{:S(2)}) async-start(f32[16,1,4096]{2,1,0:T(1,128)} %reshape.34), calls=%async_computation.2 | async-start | bytes 524288 | tf_op jit(solution)/shard_map/all_to_all | solution.py:93
  80.0 23.7 %copy-start.1 = (f32[1024]{0:T(1024)S(1)}, f32[1024]{0:T(1024)}, u32[]{:S(2)}) copy-start(f32[1024]{0:T(1024)} %param.7) | copy-start | bytes 12292
  103.9 12.4 %collective-permute-start = (bf16[26,2,1]{2,1,0:T(2,128)(2,1)S(1)}, bf16[26,2,1]{2,1,0:T(2,128)(2,1)S(1)}, u32[]{:S(2)}, u32[]{:S(2)}) collective-permute-start(bf16[26,2,1]{2,1,0:T(2,128)(2,1)S(1)} %get-tuple-element.10), channel_id=1, source_target_pairs={{0,4},{4,8},{8,12},{1,5},{5,9},{9,13},{2,6},{6,10},{10,14},{3,7},{... | collective-permute-start | bytes 320 | tf_op jit(solution)/shard_map/ppermute | solution.py:45
  114.4 8.9 %collective-permute-start.1 = (bf16[26,2,1]{2,1,0:T(2,128)(2,1)S(1)}, bf16[26,2,1]{2,1,0:T(2,128)(2,1)S(1)}, u32[]{:S(2)}, u32[]{:S(2)}) collective-permute-start(bf16[26,2,1]{2,1,0:T(2,128)(2,1)S(1)} %get-tuple-element.9), channel_id=1, source_target_pairs={{4,0},{8,4},{12,8},{5,1},{9,5},{13,9},{6,2},{10,6},{14,10},{7,3},{... | collective-permute-start | bytes 320 | tf_op jit(solution)/shard_map/ppermute | solution.py:47
